TPU v7x, 32 devices: a whole 2x2x4 slice. The times are simulated.
32 devices in a mesh: owner: 8 (over z, y), sub: 4 (over x, core).
Axes of the slice: x: 2, y: 2, z: 4, core: 2. Of those that a mesh axis runs over, the one named last changes fastest.
Arguments:
- velocity: float32 [6, 16384], P(None, 'owner'), may hold values from -6 to 6
- properties: float32 [4, 16384], P(None, 'owner'), may hold values from 0.3 to 3
- first_body: int32 [262144], P(('owner', 'sub')), may hold values from 0 to 16383, as said below
- second_body: int32 [262144], P(('owner', 'sub')), may hold values from 0 to 16383, as said below
- geometry: float32 [9, 262144], P(None, ('owner', 'sub')), may hold values from -2 to 2, as said below
- target_speed: float32 [262144], P(('owner', 'sub')), may hold values from -1 to 2
- warm_impulse: float32 [262144], P(('owner', 'sub')), may hold values from 0 to 0.5
- live_pairs: int32 [2048], P(('owner', 'sub')), may hold values from 0 to 128, as said below
Outputs:
- velocity_out: float32 [6, 16384], P(None, 'owner')
- impulse_out: float32 [262144], P(('owner', 'sub'))
Inputs may be any that keep to these rules, and one draw needn't show every extreme that they name: Pair slots are ordered by device of owner+sub, then by partner owner, then by 8 blocks of 128 slots; a slot on a device of owner o with partner owner q has first_body in [o * 2048, (o+1) * 2048) and second_body in [q * 2048, (q+1) * 2048). `second_body`: see first_body. `live_pairs`: on every device the first block toward its own owner is full; live counts differ strongly between devices and between partner owners. `geometry`: rows 0 to 2 of every column have unit length.
All inputs are finite; a program needn't handle non-finite values.
Results may differ from a plain program's by a relative error of at most 0.0001.
Values sent between devices are 32-bit elements; how exact they have to be, the bound alone decides.
A program may use at most 128 MiB of HBM per device.

v0:
```python
import functools

import jax
import jax.numpy as jnp
from jax import lax
from jax.experimental import pallas as pl
from jax.experimental.pallas import tpu as pltpu
from jax.sharding import PartitionSpec as P

ITERS = 4
LANES = 128
VEL = 6
PROPS = 4
relax = 0.1
MESH = pl.DeviceIdType.MESH


def cross_rows(left, right):
    return [
        left[1] * right[2] - left[2] * right[1],
        left[2] * right[0] - left[0] * right[2],
        left[0] * right[1] - left[1] * right[0],
    ]


def peer(position, shift, devices, subs):
    target = lax.rem(position + shift, devices)
    return target, (lax.div(target, subs), lax.rem(target, subs))


def greet(position, devices, subs):
    barrier = pltpu.get_barrier_semaphore()

    def signal(shift, carry):
        _, where = peer(position, shift, devices, subs)
        pl.semaphore_signal(barrier, inc=1, device_id=where, device_id_type=MESH)
        return carry

    lax.fori_loop(1, devices, signal, 0)
    pl.semaphore_wait(barrier, devices - 1)


def spread(position, devices, subs, source, target_ref, send_sem, recv_sem, step=1):
    def copy(shift, slot):
        _, where = peer(position, shift, devices, subs)
        return pltpu.make_async_remote_copy(
            src_ref=source,
            dst_ref=target_ref.at[slot],
            send_sem=send_sem.at[shift - 1],
            recv_sem=recv_sem.at[shift - 1],
            device_id=where,
            device_id_type=MESH,
        )

    def start(shift, carry):
        copy(shift, position).start()
        return carry

    def finish(shift, carry):
        sender = lax.rem(position - shift + devices, devices)
        copy(shift, sender).wait()
        return carry

    lax.fori_loop(1, devices, start, 0)
    lax.fori_loop(1, devices, finish, 0)


def share_kernel(devices, subs, piece_ref, full_ref, send_sem, recv_sem):
    position = lax.axis_index("owner") * subs + lax.axis_index("sub")
    full_ref[position] = piece_ref[...]
    greet(position, devices, subs)
    spread(position, devices, subs, piece_ref, full_ref, send_sem, recv_sem)


def reduce_share_kernel(
    devices, subs, delta_ref, own_ref, full_ref, piece_ref, held, send_sem, recv_sem, send2, recv2
):
    position = lax.axis_index("owner") * subs + lax.axis_index("sub")
    greet(position, devices, subs)

    def copy(shift):
        target, where = peer(position, shift, devices, subs)
        return pltpu.make_async_remote_copy(
            src_ref=delta_ref.at[target],
            dst_ref=held.at[shift - 1],
            send_sem=send_sem.at[shift - 1],
            recv_sem=recv_sem.at[shift - 1],
            device_id=where,
            device_id_type=MESH,
        )

    def start(shift, carry):
        copy(shift).start()
        return carry

    def take(shift, total):
        copy(shift).wait()
        return total + held[shift - 1]

    lax.fori_loop(1, devices, start, 0)
    total = own_ref[...] + delta_ref[position]
    total = lax.fori_loop(1, devices, take, total)
    piece_ref[...] = total
    full_ref[position] = total
    spread(position, devices, subs, piece_ref, full_ref, send2, recv2)


def comm_params(collective_id):
    return pltpu.CompilerParams(collective_id=collective_id, has_side_effects=True)


def vmem_specs(count):
    return [pl.BlockSpec(memory_space=pltpu.VMEM)] * count


def share(piece, devices, subs):
    return pl.pallas_call(
        functools.partial(share_kernel, devices, subs),
        name="share",
        out_shape=jax.ShapeDtypeStruct((devices,) + piece.shape, jnp.float32),
        in_specs=vmem_specs(1),
        out_specs=vmem_specs(1)[0],
        scratch_shapes=[pltpu.SemaphoreType.DMA((devices - 1,))] * 2,
        compiler_params=comm_params(0),
    )(piece)


def reduce_share(delta, own, devices, subs):
    return pl.pallas_call(
        functools.partial(reduce_share_kernel, devices, subs),
        name="reduce_share",
        out_shape=(
            jax.ShapeDtypeStruct(delta.shape, jnp.float32),
            jax.ShapeDtypeStruct(own.shape, jnp.float32),
        ),
        in_specs=vmem_specs(2),
        out_specs=tuple(vmem_specs(2)),
        scratch_shapes=[pltpu.VMEM((devices - 1,) + own.shape, jnp.float32)]
        + [pltpu.SemaphoreType.DMA((devices - 1,))] * 4,
        compiler_params=comm_params(1),
    )(delta, own)


def low_high(index, height):
    chunk = lax.shift_right_logical(index, 7)
    if height & (height - 1) == 0:
        chunk = chunk & (height - 1)
    else:
        chunk = lax.rem(chunk, jnp.full_like(chunk, height))
    return index & (LANES - 1), chunk


def gather_rows(table_ref, base, subs, first_row, rows, part, low, chunk):
    out = [jnp.zeros(low.shape, jnp.float32) for _ in range(rows)]
    for sub in range(subs):
        for c in range(part):
            hit = chunk == sub * part + c
            for row in range(rows):
                line = table_ref[base + sub, pl.ds((first_row + row) * part + c, 1), :]
                picked = jnp.take_along_axis(
                    jnp.broadcast_to(line, low.shape), low, axis=1, mode="promise_in_bounds"
                )
                out[row] = jnp.where(hit, picked, out[row])
    return out


def prepare_kernel(groups, subs, part, table_ref, first_ref, second_ref, geo_ref, coef_ref):
    owner = lax.axis_index("owner")

    def body(q, carry):
        low1, chunk1 = low_high(first_ref[q], subs * part)
        low2, chunk2 = low_high(second_ref[q], subs * part)
        normal = [geo_ref[k, q] for k in range(3)]
        cross1 = cross_rows([geo_ref[3 + k, q] for k in range(3)], normal)
        cross2 = cross_rows([geo_ref[6 + k, q] for k in range(3)], normal)
        props1 = gather_rows(table_ref, owner * subs, subs, VEL, PROPS, part, low1, chunk1)
        props2 = gather_rows(table_ref, q * subs, subs, VEL, PROPS, part, low2, chunk2)
        mass = props1[0] + props2[0]
        for k in range(3):
            mass += cross1[k] * cross1[k] * props1[1 + k]
            mass += cross2[k] * cross2[k] * props2[1 + k]
        values = [relax / mass] + props1 + props2
        for k, value in enumerate(values):
            coef_ref[q, k] = value
        return carry

    lax.fori_loop(0, groups, body, 0)


def place(deltas, low, chunk, height):
    rows = len(deltas)
    tall = lax.broadcasted_iota(jnp.int32, (height, LANES), 0)
    wide = lax.broadcasted_iota(jnp.int32, (LANES, LANES), 0)
    left, right = [], []
    coarse = [d.astype(jnp.bfloat16).astype(jnp.float32) for d in deltas]
    fine = [d - c for d, c in zip(deltas, coarse)]
    for i in range(low.shape[0]):
        hit = tall == jnp.broadcast_to(chunk[i : i + 1], (height, LANES))
        block = [
            jnp.where(hit, jnp.broadcast_to(x[i : i + 1], (height, LANES)), 0.0)
            for x in coarse + fine
        ]
        left.append(jnp.concatenate(block, axis=0).astype(jnp.bfloat16))
        right.append(
            jnp.where(wide == jnp.broadcast_to(low[i : i + 1], (LANES, LANES)), 1.0, 0.0).astype(
                jnp.bfloat16
            )
        )
    out = lax.dot_general(
        jnp.concatenate(left, axis=1),
        jnp.concatenate(right, axis=1),
        (((1,), (1,)), ((), ())),
        preferred_element_type=jnp.float32,
    )
    return out[: rows * height] + out[rows * height :]


def iterate_kernel(
    groups, subs, part, table_ref, first_ref, second_ref, geo_ref, coef_ref, target_ref, live_ref,
    impulse_ref, impulse_out, delta_ref, own_acc
):
    owner = lax.axis_index("owner")
    height = subs * part
    own_acc[...] = jnp.zeros_like(own_acc)

    def body(q, carry):
        low1, chunk1 = low_high(first_ref[q], height)
        low2, chunk2 = low_high(second_ref[q], height)
        normal = [geo_ref[k, q] for k in range(3)]
        cross1 = cross_rows([geo_ref[3 + k, q] for k in range(3)], normal)
        cross2 = cross_rows([geo_ref[6 + k, q] for k in range(3)], normal)
        vel1 = gather_rows(table_ref, owner * subs, subs, 0, VEL, part, low1, chunk1)
        vel2 = gather_rows(table_ref, q * subs, subs, 0, VEL, part, low2, chunk2)
        speed = jnp.zeros_like(vel1[0])
        for k in range(3):
            speed += normal[k] * (vel1[k] - vel2[k])
            speed += cross1[k] * vel1[3 + k] - cross2[k] * vel2[3 + k]
        impulse = impulse_ref[q]
        step = (target_ref[q] - speed) * coef_ref[q, 0]
        lane = lax.broadcasted_iota(jnp.int32, impulse.shape, 1)
        fresh = jnp.where(lane < live_ref[q], jnp.maximum(impulse + step, 0.0), impulse)
        impulse_out[q] = fresh
        applied = fresh - impulse
        delta1 = [coef_ref[q, 1] * applied * normal[k] for k in range(3)]
        delta1 += [coef_ref[q, 2 + k] * (applied * cross1[k]) for k in range(3)]
        delta2 = [-(coef_ref[q, 5] * applied * normal[k]) for k in range(3)]
        delta2 += [-(coef_ref[q, 6 + k] * (applied * cross2[k])) for k in range(3)]
        own_acc[...] += place(delta1, low1, chunk1, height)
        there = place(delta2, low2, chunk2, height)
        for sub in range(subs):
            for row in range(VEL):
                start = row * height + sub * part
                delta_ref[q * subs + sub, pl.ds(row * part, part), :] = there[start : start + part]
        return carry

    lax.fori_loop(0, groups, body, 0)
    for sub in range(subs):
        for row in range(VEL):
            start = row * height + sub * part
            delta_ref[owner * subs + sub, pl.ds(row * part, part), :] += own_acc[
                start : start + part, :
            ]


def on_device(
    groups, subs, velocity, properties, first_body, second_body, geometry, target_speed,
    warm_impulse, live_pairs
):
    owned = velocity.shape[1]
    devices = groups * subs
    part = owned // (LANES * subs)
    count = first_body.shape[0]
    rows = count // (groups * LANES)
    block = count // live_pairs.shape[0]
    tiles = (groups, rows, LANES)
    sub = lax.axis_index("sub")

    def own_piece(array):
        cut = lax.dynamic_slice_in_dim(array, sub * (part * LANES), part * LANES, 1)
        return cut.reshape(-1, LANES)

    own = own_piece(velocity)
    table = share(jnp.concatenate([own, own_piece(properties)], axis=0), devices, subs)
    first = first_body.reshape(tiles)
    second = second_body.reshape(tiles)
    geo = geometry.reshape((geometry.shape[0],) + tiles)
    target = target_speed.reshape(tiles)
    impulse = warm_impulse.reshape(tiles)
    slot = jnp.arange(LANES, dtype=jnp.int32)
    rows_per_block = block // LANES
    offset = jnp.arange(count // LANES, dtype=jnp.int32) % rows_per_block * LANES
    bound = jnp.repeat(live_pairs, rows_per_block, total_repeat_length=count // LANES) - offset
    live = jnp.broadcast_to(bound[:, None], (count // LANES, LANES)).reshape(tiles)

    coef = pl.pallas_call(
        functools.partial(prepare_kernel, groups, subs, part),
        name="prepare",
        out_shape=jax.ShapeDtypeStruct((groups, 9, rows, LANES), jnp.float32),
        in_specs=vmem_specs(4),
        out_specs=vmem_specs(1)[0],
    )(table, first, second, geo)

    step = pl.pallas_call(
        functools.partial(iterate_kernel, groups, subs, part),
        name="iterate",
        out_shape=(
            jax.ShapeDtypeStruct(tiles, jnp.float32),
            jax.ShapeDtypeStruct((devices, VEL * part, LANES), jnp.float32),
        ),
        in_specs=vmem_specs(8),
        out_specs=tuple(vmem_specs(2)),
        scratch_shapes=[pltpu.VMEM((VEL * subs * part, LANES), jnp.float32)],
    )
    for _ in range(ITERS):
        impulse, delta = step(table, first, second, geo, coef, target, live, impulse)
        table, own = reduce_share(delta, own, devices, subs)
    start = lax.axis_index("owner") * subs
    mine = lax.dynamic_slice_in_dim(table, start, subs, 0).reshape(subs, VEL, part, LANES)
    speeds = mine.transpose(1, 0, 2, 3).reshape(VEL, owned)
    return (speeds, impulse.reshape(count))


def solution(mesh):
    groups, subs = mesh.shape["owner"], mesh.shape["sub"]
    return jax.shard_map(
        functools.partial(on_device, groups, subs),
        mesh=mesh,
        in_specs=(
            P(None, "owner"),
            P(None, "owner"),
            P(("owner", "sub")),
            P(("owner", "sub")),
            P(None, ("owner", "sub")),
            P(("owner", "sub")),
            P(("owner", "sub")),
            P(("owner", "sub")),
        ),
        out_specs=(P(None, "owner"), P(("owner", "sub"))),
        check_vma=False,
    )
```

profile of v0, /device:TPU:0, one launch (start us, length us, event | category | flops | bytes accessed | tf_op | source)
XLA Modules:
  0.0 171.0 jit_solution(8226697354339388059)
XLA Ops:
  0.6 0.0 copy-start
  0.7 0.0 copy-start.1
  0.7 0.0 copy-start.2
  0.7 0.6 copy-done.1
  1.3 0.8 gather_fusion
  2.1 0.1 broadcast_in_dim.8
  2.2 0.7 constant_dynamic-slice_fusion.1
  2.9 0.0 copy-done
  2.9 0.0 copy-start.3
  3.0 0.6 pad_maximum_fusion.piece_ref
  3.6 0.0 copy-done.3
  3.6 0.7 broadcast_in_dim.14.live_ref
  4.3 0.0 copy-done.2
  4.3 0.1 copy.11
  4.4 0.7 slice_bitcast_fusion.geo_ref
  5.1 20.2 %share.1.table_ref = f32[32,40,128]{2,1,0:T(8,128)} custom-call(f32[40,128]{1,0:T(8,128)} %pad_maximum_fusion.piece_ref), custom_call_target="tpu_custom_call" | custom-call | tf_op jit(solution)/shard_map/share/pallas_call | solution.py:117
  25.3 3.7 %prepare.1.coef_ref = f32[8,9,8,128]{3,2,1,0:T(8,128)} custom-call(f32[32,40,128]{2,1,0:T(8,128)} %share.1.table_ref, s32[8,8,128]{2,1,0:T(8,128)} %bitcast.14, s32[8,8,128]{2,1,0:T(8,128)} %bitcast.19, f32[9,8,8,128]{3,2,1,0:T(8,128)} %slice_bitcast_fusion.geo_ref), custom_call_target="tpu_custom_call" | custom-call | tf_op jit(solution)/shard_map/prepare/pallas_call | solution.py:295
  29.0 8.1 %iterate.4 = (f32[8,8,128]{2,1,0:T(8,128)}, f32[32,24,128]{2,1,0:T(8,128)}) custom-call(f32[32,40,128]{2,1,0:T(8,128)} %share.1.table_ref, s32[8,8,128]{2,1,0:T(8,128)} %bitcast.15, s32[8,8,128]{2,1,0:T(8,128)} %bitcast.20, f32[9,8,8,128]{3,2,1,0:T(8,128)} %slice_bitcast_fusion.geo_ref, f32[8,9,8,128]{3,2,1,0:T(8,128)} %prepare.1.coef_ref, ...), custom_call_target="tpu_custom_call" | custom-call | tf_op jit(solution)/shard_map/iterate/pallas_call | solution.py:315
  37.0 27.6 %reduce_share.4 = (f32[32,24,128]{2,1,0:T(8,128)}, f32[24,128]{1,0:T(8,128)}) custom-call(f32[32,24,128]{2,1,0:T(8,128)} %get-tuple-element.29.delta_ref, f32[24,128]{1,0:T(8,128)} %copy-done.3), custom_call_target="tpu_custom_call" | custom-call | tf_op jit(solution)/shard_map/reduce_share/pallas_call | solution.py:129
  64.6 8.0 %iterate.5 = (f32[8,8,128]{2,1,0:T(8,128)}, f32[32,24,128]{2,1,0:T(8,128)}) custom-call(f32[32,24,128]{2,1,0:T(8,128)} %get-tuple-element.30.table_ref, s32[8,8,128]{2,1,0:T(8,128)} %bitcast.16, s32[8,8,128]{2,1,0:T(8,128)} %bitcast.21, f32[9,8,8,128]{3,2,1,0:T(8,128)} %slice_bitcast_fusion.geo_ref, f32[8,9,8,128]{3,2,1,0:T(8,128)} %prepare.1.coef_ref, ...), custom_call_target="tpu_custom_call" | custom-call | tf_op jit(solution)/shard_map/iterate/pallas_call | solution.py:315
  72.6 26.9 %reduce_share.5 = (f32[32,24,128]{2,1,0:T(8,128)}, f32[24,128]{1,0:T(8,128)}) custom-call(f32[32,24,128]{2,1,0:T(8,128)} %get-tuple-element.32.delta_ref, f32[24,128]{1,0:T(8,128)} %get-tuple-element.33.own_ref), custom_call_target="tpu_custom_call" | custom-call | tf_op jit(solution)/shard_map/reduce_share/pallas_call | solution.py:129
  99.5 8.0 %iterate.6 = (f32[8,8,128]{2,1,0:T(8,128)}, f32[32,24,128]{2,1,0:T(8,128)}) custom-call(f32[32,24,128]{2,1,0:T(8,128)} %get-tuple-element.34.table_ref, s32[8,8,128]{2,1,0:T(8,128)} %bitcast.17, s32[8,8,128]{2,1,0:T(8,128)} %bitcast.22, f32[9,8,8,128]{3,2,1,0:T(8,128)} %slice_bitcast_fusion.geo_ref, f32[8,9,8,128]{3,2,1,0:T(8,128)} %prepare.1.coef_ref, ...), custom_call_target="tpu_custom_call" | custom-call | tf_op jit(solution)/shard_map/iterate/pallas_call | solution.py:315
  107.5 27.1 %reduce_share.6 = (f32[32,24,128]{2,1,0:T(8,128)}, f32[24,128]{1,0:T(8,128)}) custom-call(f32[32,24,128]{2,1,0:T(8,128)} %get-tuple-element.36.delta_ref, f32[24,128]{1,0:T(8,128)} %get-tuple-element.37.own_ref), custom_call_target="tpu_custom_call" | custom-call | tf_op jit(solution)/shard_map/reduce_share/pallas_call | solution.py:129
  134.6 8.0 %iterate.7 = (f32[8,8,128]{2,1,0:T(8,128)}, f32[32,24,128]{2,1,0:T(8,128)}) custom-call(f32[32,24,128]{2,1,0:T(8,128)} %get-tuple-element.38.table_ref, s32[8,8,128]{2,1,0:T(8,128)} %bitcast.18, s32[8,8,128]{2,1,0:T(8,128)} %bitcast.23, f32[9,8,8,128]{3,2,1,0:T(8,128)} %slice_bitcast_fusion.geo_ref, f32[8,9,8,128]{3,2,1,0:T(8,128)} %prepare.1.coef_ref, ...), custom_call_target="tpu_custom_call" | custom-call | tf_op jit(solution)/shard_map/iterate/pallas_call | solution.py:315
  142.6 26.9 %reduce_share.7 = (f32[32,24,128]{2,1,0:T(8,128)}, f32[24,128]{1,0:T(8,128)}) custom-call(f32[32,24,128]{2,1,0:T(8,128)} %get-tuple-element.40.delta_ref, f32[24,128]{1,0:T(8,128)} %get-tuple-element.41.own_ref), custom_call_target="tpu_custom_call" | custom-call | tf_op jit(solution)/shard_map/reduce_share/pallas_call | solution.py:129
  169.5 0.8 constant_dynamic-slice_fusion
  170.4 0.7 reshape.85
  (6 shorter events, 0.0 us)
Async XLA Ops:
  0.6 2.3 %copy-start = (f32[6,2048]{1,0:T(8,128)S(1)}, f32[6,2048]{1,0:T(8,128)}, u32[]{:S(2)}) copy-start(f32[6,2048]{1,0:T(8,128)} %param.10) | copy-start | bytes 147460
  0.7 0.7 copy-start.1
  0.7 3.6 %copy-start.2 = (f32[9,8192]{1,0:T(8,128)S(1)}, f32[9,8192]{1,0:T(8,128)}, u32[]{:S(2)}) copy-start(f32[9,8192]{1,0:T(8,128)} %param.14) | copy-start | bytes 884740
  2.9 0.6 copy-start.3
where the time goes:
time: 173 us; the launch traced here: 171 us
  Pallas kernels  164 us (95%)
  local copies, waits for them, and re-layouts  5.26 us (3%)
    pallas_call x4, Pallas kernels, reduce_share(): pl.pallas_call(functools.partial(reduce_share_kernel, devices, subs), nam...  108 us
    pallas_call x4, Pallas kernels, on_device(): step(table, first, second, geo, coef, target, live, impulse)  32.1 us
    pallas_call x1, Pallas kernels, share(): pl.pallas_call(functools.partial(share_kernel, devices, subs), name='shar...  20.2 us
    pallas_call x1, Pallas kernels, on_device(): pl.pallas_call(functools.partial(prepare_kernel, groups, subs, part), nam...  3.66 us

commit v1 on v0

--- a/solution.py
+++ b/solution.py
@@ -23,86 +23,153 @@
     ]
 
 
-def peer(position, shift, devices, subs):
-    target = lax.rem(position + shift, devices)
-    return target, (lax.div(target, subs), lax.rem(target, subs))
-
-
-def greet(position, devices, subs):
+def around(index, shift, size):
+    return lax.rem(index + shift + size, size)
+
+
+def greet(groups, subs, owner, sub):
     barrier = pltpu.get_barrier_semaphore()
 
     def signal(shift, carry):
-        _, where = peer(position, shift, devices, subs)
+        where = (around(owner, shift, groups), sub)
         pl.semaphore_signal(barrier, inc=1, device_id=where, device_id_type=MESH)
         return carry
 
-    lax.fori_loop(1, devices, signal, 0)
-    pl.semaphore_wait(barrier, devices - 1)
-
-
-def spread(position, devices, subs, source, target_ref, send_sem, recv_sem, step=1):
-    def copy(shift, slot):
-        _, where = peer(position, shift, devices, subs)
-        return pltpu.make_async_remote_copy(
-            src_ref=source,
-            dst_ref=target_ref.at[slot],
-            send_sem=send_sem.at[shift - 1],
-            recv_sem=recv_sem.at[shift - 1],
-            device_id=where,
-            device_id_type=MESH,
+    lax.fori_loop(1, groups, signal, 0)
+    for j in range(1, subs):
+        where = (owner, around(sub, j, subs))
+        pl.semaphore_signal(barrier, inc=1, device_id=where, device_id_type=MESH)
+    pl.semaphore_wait(barrier, groups + subs - 2)
+
+
+def remote(source, target, send_sem, recv_sem, where):
+    return pltpu.make_async_remote_copy(
+        src_ref=source,
+        dst_ref=target,
+        send_sem=send_sem,
+        recv_sem=recv_sem,
+        device_id=where,
+        device_id_type=MESH,
+    )
+
+
+def gather_all(groups, subs, owner, sub, piece_ref, full_ref, send3, recv3, send4, recv4):
+    def across(k, slot):
+        where = (around(owner, k, groups), sub)
+        return remote(piece_ref, full_ref.at[slot], send3.at[k - 1], recv3.at[k - 1], where)
+
+    def along(j, k, source, slot):
+        where = (owner, around(sub, j, subs))
+        return remote(source, full_ref.at[slot], send4.at[j - 1, k], recv4.at[j - 1, k], where)
+
+    def start(k, carry):
+        across(k, owner * subs + sub).start()
+        return carry
+
+    def relay(k, carry):
+        slot = around(owner, -k, groups) * subs + sub
+        across(k, slot).wait_recv()
+        for j in range(1, subs):
+            along(j, k, full_ref.at[slot], slot).start()
+        return carry
+
+    def finish(k, carry):
+        for j in range(1, subs):
+            slot = around(owner, -k, groups) * subs + around(sub, -j, subs)
+            along(j, k, piece_ref, slot).wait()
+        return carry
+
+    def sent(k, carry):
+        across(k, owner * subs + sub).wait_send()
+        return carry
+
+    lax.fori_loop(1, groups, start, 0)
+    for j in range(1, subs):
+        along(j, 0, piece_ref, owner * subs + sub).start()
+    lax.fori_loop(1, groups, relay, 0)
+    lax.fori_loop(0, groups, finish, 0)
+    lax.fori_loop(1, groups, sent, 0)
+
+
+def share_kernel(groups, subs, piece_ref, full_ref, send3, recv3, send4, recv4):
+    owner, sub = lax.axis_index("owner"), lax.axis_index("sub")
+    full_ref[owner * subs + sub] = piece_ref[...]
+    greet(groups, subs, owner, sub)
+    gather_all(groups, subs, owner, sub, piece_ref, full_ref, send3, recv3, send4, recv4)
+
+
+def reduce_share_kernel(
+    groups, subs, last, delta_ref, own_ref, full_ref, piece_ref, held1, held2, reduced,
+    send1, recv1, send2, recv2, send3, recv3, send4, recv4
+):
+    owner, sub = lax.axis_index("owner"), lax.axis_index("sub")
+    greet(groups, subs, owner, sub)
+
+    def inner(k, j):
+        q, there = around(owner, k, groups), around(sub, j, subs)
+        return remote(
+            delta_ref.at[q * subs + there],
+            held1.at[j - 1, k],
+            send1.at[j - 1, k],
+            recv1.at[j - 1, k],
+            (owner, there),
         )
 
-    def start(shift, carry):
-        copy(shift, position).start()
-        return carry
-
-    def finish(shift, carry):
-        sender = lax.rem(position - shift + devices, devices)
-        copy(shift, sender).wait()
-        return carry
-
-    lax.fori_loop(1, devices, start, 0)
-    lax.fori_loop(1, devices, finish, 0)
-
-
-def share_kernel(devices, subs, piece_ref, full_ref, send_sem, recv_sem):
-    position = lax.axis_index("owner") * subs + lax.axis_index("sub")
-    full_ref[position] = piece_ref[...]
-    greet(position, devices, subs)
-    spread(position, devices, subs, piece_ref, full_ref, send_sem, recv_sem)
-
-
-def reduce_share_kernel(
-    devices, subs, delta_ref, own_ref, full_ref, piece_ref, held, send_sem, recv_sem, send2, recv2
-):
-    position = lax.axis_index("owner") * subs + lax.axis_index("sub")
-    greet(position, devices, subs)
-
-    def copy(shift):
-        target, where = peer(position, shift, devices, subs)
-        return pltpu.make_async_remote_copy(
-            src_ref=delta_ref.at[target],
-            dst_ref=held.at[shift - 1],
-            send_sem=send_sem.at[shift - 1],
-            recv_sem=recv_sem.at[shift - 1],
-            device_id=where,
-            device_id_type=MESH,
+    def outer(k):
+        where = (around(owner, k, groups), sub)
+        return remote(
+            reduced.at[k - 1], held2.at[k - 1], send2.at[k - 1], recv2.at[k - 1], where
         )
 
-    def start(shift, carry):
-        copy(shift).start()
-        return carry
-
-    def take(shift, total):
-        copy(shift).wait()
-        return total + held[shift - 1]
-
-    lax.fori_loop(1, devices, start, 0)
-    total = own_ref[...] + delta_ref[position]
-    total = lax.fori_loop(1, devices, take, total)
+    def start(k, carry):
+        for j in range(1, subs):
+            inner(k, j).start()
+        return carry
+
+    def summed(k):
+        total = delta_ref[around(owner, k, groups) * subs + sub]
+        for j in range(1, subs):
+            inner(k, j).wait_recv()
+            total += held1[j - 1, k]
+        return total
+
+    def pass_on(k, carry):
+        reduced[k - 1] = summed(k)
+        outer(k).start()
+        return carry
+
+    def take(k, total):
+        outer(k).wait()
+        return total + held2[k - 1]
+
+    def sent(k, carry):
+        for j in range(1, subs):
+            inner(k, j).wait_send()
+        return carry
+
+    lax.fori_loop(1, groups, start, 0)
+    start(0, 0)
+    lax.fori_loop(1, groups, pass_on, 0)
+    total = own_ref[...] + summed(0)
+    total = lax.fori_loop(1, groups, take, total)
+    lax.fori_loop(0, groups, sent, 0)
     piece_ref[...] = total
-    full_ref[position] = total
-    spread(position, devices, subs, piece_ref, full_ref, send2, recv2)
+    if last:
+        full_ref[sub] = total
+
+        def along(j, slot):
+            where = (owner, around(sub, j, subs))
+            return remote(
+                piece_ref, full_ref.at[slot], send4.at[j - 1, 0], recv4.at[j - 1, 0], where
+            )
+
+        for j in range(1, subs):
+            along(j, sub).start()
+        for j in range(1, subs):
+            along(j, around(sub, -j, subs)).wait()
+    else:
+        full_ref[owner * subs + sub] = total
+        gather_all(groups, subs, owner, sub, piece_ref, full_ref, send3, recv3, send4, recv4)
 
 
 def comm_params(collective_id):
@@ -113,31 +180,43 @@
     return [pl.BlockSpec(memory_space=pltpu.VMEM)] * count
 
 
-def share(piece, devices, subs):
+def semaphores(groups, subs, wide):
+    shape = (subs - 1, groups) if wide else (groups - 1,)
+    return [pltpu.SemaphoreType.DMA(shape)] * 2
+
+
+def share(piece, groups, subs):
     return pl.pallas_call(
-        functools.partial(share_kernel, devices, subs),
+        functools.partial(share_kernel, groups, subs),
         name="share",
-        out_shape=jax.ShapeDtypeStruct((devices,) + piece.shape, jnp.float32),
+        out_shape=jax.ShapeDtypeStruct((groups * subs,) + piece.shape, jnp.float32),
         in_specs=vmem_specs(1),
         out_specs=vmem_specs(1)[0],
-        scratch_shapes=[pltpu.SemaphoreType.DMA((devices - 1,))] * 2,
+        scratch_shapes=semaphores(groups, subs, False) + semaphores(groups, subs, True),
         compiler_params=comm_params(0),
     )(piece)
 
 
-def reduce_share(delta, own, devices, subs):
+def reduce_share(delta, own, groups, subs, last):
+    pieces = subs if last else groups * subs
     return pl.pallas_call(
-        functools.partial(reduce_share_kernel, devices, subs),
-        name="reduce_share",
+        functools.partial(reduce_share_kernel, groups, subs, last),
+        name="reduce_last" if last else "reduce_share",
         out_shape=(
-            jax.ShapeDtypeStruct(delta.shape, jnp.float32),
+            jax.ShapeDtypeStruct((pieces,) + own.shape, jnp.float32),
             jax.ShapeDtypeStruct(own.shape, jnp.float32),
         ),
         in_specs=vmem_specs(2),
         out_specs=tuple(vmem_specs(2)),
-        scratch_shapes=[pltpu.VMEM((devices - 1,) + own.shape, jnp.float32)]
-        + [pltpu.SemaphoreType.DMA((devices - 1,))] * 4,
-        compiler_params=comm_params(1),
+        scratch_shapes=[
+            pltpu.VMEM((subs - 1, groups) + own.shape, jnp.float32),
+            pltpu.VMEM((groups - 1,) + own.shape, jnp.float32),
+            pltpu.VMEM((groups - 1,) + own.shape, jnp.float32),
+        ]
+        + semaphores(groups, subs, True)
+        + semaphores(groups, subs, False) * 2
+        + semaphores(groups, subs, True),
+        compiler_params=comm_params(2 if last else 1),
     )(delta, own)
 
 
@@ -280,7 +359,7 @@
         return cut.reshape(-1, LANES)
 
     own = own_piece(velocity)
-    table = share(jnp.concatenate([own, own_piece(properties)], axis=0), devices, subs)
+    table = share(jnp.concatenate([own, own_piece(properties)], axis=0), groups, subs)
     first = first_body.reshape(tiles)
     second = second_body.reshape(tiles)
     geo = geometry.reshape((geometry.shape[0],) + tiles)
@@ -311,11 +390,10 @@
         out_specs=tuple(vmem_specs(2)),
         scratch_shapes=[pltpu.VMEM((VEL * subs * part, LANES), jnp.float32)],
     )
-    for _ in range(ITERS):
+    for iteration in range(ITERS):
         impulse, delta = step(table, first, second, geo, coef, target, live, impulse)
-        table, own = reduce_share(delta, own, devices, subs)
-    start = lax.axis_index("owner") * subs
-    mine = lax.dynamic_slice_in_dim(table, start, subs, 0).reshape(subs, VEL, part, LANES)
+        table, own = reduce_share(delta, own, groups, subs, iteration == ITERS - 1)
+    mine = table.reshape(subs, VEL, part, LANES)
     speeds = mine.transpose(1, 0, 2, 3).reshape(VEL, owned)
     return (speeds, impulse.reshape(count))
 

time: 173 us -> 144 us (0.83)
  Pallas kernels: 164 us -> 137 us
    pallas_call x5, Pallas kernels: 129 us -> 101 us  [the longest x4 83.1 us: reduce_share(): pl.pallas_call(functools.partial(reduce_share_kernel, groups, subs, last)...]
where the time goes in v1:
time: 144 us; the launch traced here: 143 us
  Pallas kernels  137 us (95%)
  local copies, waits for them, and re-layouts  5.25 us (4%)
    pallas_call x4, Pallas kernels, reduce_share(): pl.pallas_call(functools.partial(reduce_share_kernel, groups, subs, last)...  83.1 us
    pallas_call x4, Pallas kernels, on_device(): step(table, first, second, geo, coef, target, live, impulse)  32.1 us
    pallas_call x1, Pallas kernels, share(): pl.pallas_call(functools.partial(share_kernel, groups, subs), name='share...  18.1 us
    pallas_call x1, Pallas kernels, on_device(): pl.pallas_call(functools.partial(prepare_kernel, groups, subs, part), nam...  3.66 us

profile of v1, /device:TPU:0, one launch (start us, length us, event | category | flops | bytes accessed | tf_op | source)
XLA Modules:
  0.0 143.5 jit_solution(15179528449244120395)
XLA Ops:
  0.6 0.0 copy-start
  0.7 0.0 copy-start.1
  0.7 0.0 copy-start.2
  0.7 0.7 copy-done.1
  1.3 0.8 gather_fusion
  2.1 0.1 broadcast_in_dim.8
  2.2 0.7 constant_dynamic-slice_fusion
  2.9 0.0 copy-done
  2.9 0.0 copy-start.3
  3.0 0.6 pad_maximum_fusion.piece_ref
  3.6 0.0 copy-done.3
  3.6 0.7 broadcast_in_dim.14.live_ref
  4.3 0.0 copy-done.2
  4.3 0.1 copy.12
  4.4 0.7 slice_bitcast_fusion.geo_ref
  5.1 18.1 %share.1.table_ref = f32[32,40,128]{2,1,0:T(8,128)} custom-call(f32[40,128]{1,0:T(8,128)} %pad_maximum_fusion.piece_ref), custom_call_target="tpu_custom_call" | custom-call | tf_op jit(solution)/shard_map/share/pallas_call | solution.py:189
  23.2 3.7 %prepare.1.coef_ref = f32[8,9,8,128]{3,2,1,0:T(8,128)} custom-call(f32[32,40,128]{2,1,0:T(8,128)} %share.1.table_ref, s32[8,8,128]{2,1,0:T(8,128)} %bitcast.14, s32[8,8,128]{2,1,0:T(8,128)} %bitcast.19, f32[9,8,8,128]{3,2,1,0:T(8,128)} %slice_bitcast_fusion.geo_ref), custom_call_target="tpu_custom_call" | custom-call | tf_op jit(solution)/shard_map/prepare/pallas_call | solution.py:374
  26.9 8.1 %iterate.4 = (f32[8,8,128]{2,1,0:T(8,128)}, f32[32,24,128]{2,1,0:T(8,128)}) custom-call(f32[32,40,128]{2,1,0:T(8,128)} %share.1.table_ref, s32[8,8,128]{2,1,0:T(8,128)} %bitcast.15, s32[8,8,128]{2,1,0:T(8,128)} %bitcast.20, f32[9,8,8,128]{3,2,1,0:T(8,128)} %slice_bitcast_fusion.geo_ref, f32[8,9,8,128]{3,2,1,0:T(8,128)} %prepare.1.coef_ref, ...), custom_call_target="tpu_custom_call" | custom-call | tf_op jit(solution)/shard_map/iterate/pallas_call | solution.py:394
  34.9 23.0 %reduce_share.3 = (f32[32,24,128]{2,1,0:T(8,128)}, f32[24,128]{1,0:T(8,128)}) custom-call(f32[32,24,128]{2,1,0:T(8,128)} %get-tuple-element.29.delta_ref, f32[24,128]{1,0:T(8,128)} %copy-done.3), custom_call_target="tpu_custom_call" | custom-call | tf_op jit(solution)/shard_map/reduce_share/pallas_call | solution.py:202
  57.9 8.0 %iterate.5 = (f32[8,8,128]{2,1,0:T(8,128)}, f32[32,24,128]{2,1,0:T(8,128)}) custom-call(f32[32,24,128]{2,1,0:T(8,128)} %get-tuple-element.30.table_ref, s32[8,8,128]{2,1,0:T(8,128)} %bitcast.16, s32[8,8,128]{2,1,0:T(8,128)} %bitcast.21, f32[9,8,8,128]{3,2,1,0:T(8,128)} %slice_bitcast_fusion.geo_ref, f32[8,9,8,128]{3,2,1,0:T(8,128)} %prepare.1.coef_ref, ...), custom_call_target="tpu_custom_call" | custom-call | tf_op jit(solution)/shard_map/iterate/pallas_call | solution.py:394
  65.9 22.3 %reduce_share.4 = (f32[32,24,128]{2,1,0:T(8,128)}, f32[24,128]{1,0:T(8,128)}) custom-call(f32[32,24,128]{2,1,0:T(8,128)} %get-tuple-element.32.delta_ref, f32[24,128]{1,0:T(8,128)} %get-tuple-element.33.own_ref), custom_call_target="tpu_custom_call" | custom-call | tf_op jit(solution)/shard_map/reduce_share/pallas_call | solution.py:202
  88.2 8.0 %iterate.6 = (f32[8,8,128]{2,1,0:T(8,128)}, f32[32,24,128]{2,1,0:T(8,128)}) custom-call(f32[32,24,128]{2,1,0:T(8,128)} %get-tuple-element.34.table_ref, s32[8,8,128]{2,1,0:T(8,128)} %bitcast.17, s32[8,8,128]{2,1,0:T(8,128)} %bitcast.22, f32[9,8,8,128]{3,2,1,0:T(8,128)} %slice_bitcast_fusion.geo_ref, f32[8,9,8,128]{3,2,1,0:T(8,128)} %prepare.1.coef_ref, ...), custom_call_target="tpu_custom_call" | custom-call | tf_op jit(solution)/shard_map/iterate/pallas_call | solution.py:394
  96.3 22.1 %reduce_share.5 = (f32[32,24,128]{2,1,0:T(8,128)}, f32[24,128]{1,0:T(8,128)}) custom-call(f32[32,24,128]{2,1,0:T(8,128)} %get-tuple-element.36.delta_ref, f32[24,128]{1,0:T(8,128)} %get-tuple-element.37.own_ref), custom_call_target="tpu_custom_call" | custom-call | tf_op jit(solution)/shard_map/reduce_share/pallas_call | solution.py:202
  118.4 8.0 %iterate.7 = (f32[8,8,128]{2,1,0:T(8,128)}, f32[32,24,128]{2,1,0:T(8,128)}) custom-call(f32[32,24,128]{2,1,0:T(8,128)} %get-tuple-element.38.table_ref, s32[8,8,128]{2,1,0:T(8,128)} %bitcast.18, s32[8,8,128]{2,1,0:T(8,128)} %bitcast.23, f32[9,8,8,128]{3,2,1,0:T(8,128)} %slice_bitcast_fusion.geo_ref, f32[8,9,8,128]{3,2,1,0:T(8,128)} %prepare.1.coef_ref, ...), custom_call_target="tpu_custom_call" | custom-call | tf_op jit(solution)/shard_map/iterate/pallas_call | solution.py:394
  126.4 15.7 %reduce_last.1 = (f32[4,24,128]{2,1,0:T(8,128)}, f32[24,128]{1,0:T(8,128)}) custom-call(f32[32,24,128]{2,1,0:T(8,128)} %get-tuple-element.40.delta_ref, f32[24,128]{1,0:T(8,128)} %get-tuple-element.41.own_ref), custom_call_target="tpu_custom_call" | custom-call | tf_op jit(solution)/shard_map/reduce_last/pallas_call | solution.py:202
  142.0 0.8 copy.11
  142.8 0.6 reshape.85
  (5 shorter events, 0.0 us)
Async XLA Ops:
  0.6 2.3 %copy-start = (f32[6,2048]{1,0:T(8,128)S(1)}, f32[6,2048]{1,0:T(8,128)}, u32[]{:S(2)}) copy-start(f32[6,2048]{1,0:T(8,128)} %param.10) | copy-start | bytes 147460
  0.7 0.7 copy-start.1
  0.7 3.6 %copy-start.2 = (f32[9,8192]{1,0:T(8,128)S(1)}, f32[9,8192]{1,0:T(8,128)}, u32[]{:S(2)}) copy-start(f32[9,8192]{1,0:T(8,128)} %param.14) | copy-start | bytes 884740
  2.9 0.6 copy-start.3
